TPU v7x, 32 devices: a whole 2x2x4 slice. The times are simulated.
32 devices in a mesh: bvec: 4 (over y, x), row: 2 (over core), col: 4 (over z).
Axes of the slice: x: 2, y: 2, z: 4, core: 2. Of those that a mesh axis runs over, the one named last changes fastest.
Arguments:
- m_matrices: float32 [4, 2, 2048, 2048], P('bvec', None, 'row', 'col'), may hold values from -2 to 2, as said below
- bvec_index: int32 [4], replicated, may hold values from 0 to 5
- weight_table: float32 [6], replicated, may hold values from 0.25 to 2
- grad_prev: float32 [2048, 2048], P('row', 'col'), may hold values from -4 to 4, as said below
- dir_prev: float32 [2048, 2048], P('row', 'col'), may hold values from -4 to 4, as said below
Outputs:
- spread: float32 [], replicated
- trial_spread: float32 [], replicated
- gradient: float32 [2048, 2048], P('row', 'col')
- direction: float32 [2048, 2048], P('row', 'col')
- trial_diag: float32 [4, 2, 2048], replicated
Inputs may be any that keep to these rules, and one draw needn't show every extreme that they name: Each matrix m_matrices[b, p] is symmetric. grad_prev is antisymmetric. dir_prev is antisymmetric.
All inputs are finite; a program needn't handle non-finite values.
Results may differ from a plain program's by a relative error of at most 0.0003.
Values sent between devices are 32-bit elements; how exact they have to be, the bound alone decides.
A program may use at most 128 MiB of HBM per device.

v0:
```python
import jax
import jax.numpy as jnp
from jax import lax
from jax.sharding import PartitionSpec as P

TAYLOR = 8


STEP_SCALE = 1.75
HIGHEST = lax.Precision.HIGHEST


def product(left, right):
    return jnp.dot(left, right, precision=HIGHEST, preferred_element_type=jnp.float32)


def lookup_weights(bvec_index, weight_table):
    table_slots = jnp.arange(weight_table.shape[0], dtype=jnp.int32)
    return jnp.sum(
        jnp.where(table_slots[None, :] == bvec_index[:, None], weight_table[None, :], 0.0), axis=1
    )


def shards(m_matrices, bvec_index, weight_table, grad_prev, dir_prev):
    per_group = m_matrices.shape[0]
    local_rows = m_matrices.shape[2]
    local_cols = m_matrices.shape[3]
    matrix_order = local_rows * lax.axis_size("row")
    group_index = lax.axis_index("bvec")
    row_start = lax.axis_index("row") * local_rows
    col_start = lax.axis_index("col") * local_cols
    weight_all = lookup_weights(bvec_index, weight_table)
    weight_own = lax.dynamic_slice_in_dim(weight_all, group_index * per_group, per_group)
    row_ids = row_start + jnp.arange(local_rows, dtype=jnp.int32)
    col_ids = col_start + jnp.arange(local_cols, dtype=jnp.int32)
    on_diag = (row_ids[:, None] == col_ids[None, :]).astype(jnp.float32)
    own_diag = jnp.sum(m_matrices * on_diag, axis=2)
    share_diag = lax.psum(own_diag, "row")
    diagonal = lax.all_gather(share_diag, "col", axis=2, tiled=True)
    row_diag = lax.dynamic_slice_in_dim(diagonal, row_start, local_rows, 2)
    spread_own = (
        jnp.sum(weight_own[:, None] * (1.0 - diagonal[:, 0] ** 2 - diagonal[:, 1] ** 2))
        / matrix_order
    )
    leader = (lax.axis_index("row") == 0) & (lax.axis_index("col") == 0)
    spread_term = jnp.where(leader, spread_own, 0.0)
    differ = row_diag[:, :, :, None] - share_diag[:, :, None, :]
    weighted = 2.0 * weight_own[:, None, None] * jnp.sum(m_matrices * differ, axis=1)
    grad_part = jnp.sum(weighted, axis=0)
    gradient = lax.psum(grad_part, "bvec")
    counted = jnp.where(group_index == 0, 1.0, 0.0)
    grad_square = counted * jnp.sum(gradient * gradient)
    prev_square = counted * jnp.sum(grad_prev * grad_prev)
    cross_term = counted * jnp.sum(gradient * dir_prev)
    dir_square = counted * jnp.sum(dir_prev * dir_prev)
    totals = lax.psum(
        (spread_term, grad_square, prev_square, cross_term, dir_square), ("bvec", "row", "col")
    )
    spread = totals[0]
    beta_factor = totals[1] / (1.0 + totals[2])
    direction = beta_factor * dir_prev - gradient
    dir_norm = jnp.maximum(
        totals[1] - 2.0 * beta_factor * totals[3] + beta_factor * beta_factor * totals[4], 0.0
    )
    generator = STEP_SCALE * direction / jnp.sqrt(1.0 + dir_norm / matrix_order)
    block_ids = col_start + jnp.arange(local_cols, dtype=jnp.int32)
    eye_block = (row_ids[:, None] == block_ids[None, :]).astype(jnp.float32)
    horner_start = eye_block + generator / TAYLOR
    columns = lax.all_gather(generator, "row", axis=0, tiled=True)

    def accumulate(section):
        return product(section, columns)

    def horner_step(counter, current):
        folded = accumulate(lax.all_gather(current, "col", axis=1, tiled=True))
        divisor = (TAYLOR - 1 - counter).astype(jnp.float32)
        return eye_block + folded / divisor

    expmap = lax.fori_loop(0, TAYLOR - 1, horner_step, horner_start)
    expmap_cols = lax.all_gather(expmap, "row", axis=0, tiled=True)
    section = lax.all_gather(m_matrices, "col", axis=3, tiled=True)
    flattened = section.reshape((-1, section.shape[3]))
    rotated = product(flattened, expmap_cols).reshape(
        jnp.zeros(m_matrices.shape, jnp.float32).shape
    )
    trial_part = jnp.sum(expmap[None, None] * rotated, axis=2)
    trial_share = lax.psum(trial_part, "row")
    trial_group = lax.all_gather(trial_share, "col", axis=2, tiled=True)
    trial_diag = lax.all_gather(trial_group, "bvec", axis=0, tiled=True)
    trial_spread = (
        jnp.sum(weight_all[:, None] * (1.0 - trial_diag[:, 0] ** 2 - trial_diag[:, 1] ** 2))
        / matrix_order
    )
    return (spread, trial_spread, gradient, direction, trial_diag)


def solution(mesh):
    placed = (P("bvec", None, "row", "col"), P(), P(), P("row", "col"), P("row", "col"))
    return jax.shard_map(
        shards,
        mesh=mesh,
        in_specs=placed,
        out_specs=(P(), P(), P("row", "col"), P("row", "col"), P()),
        check_vma=False,
    )
```

profile of v0, /device:TPU:0, one launch (start us, length us, event | category | flops | bytes accessed | tf_op | source)
XLA Modules:
  0.0 1767.3 jit_solution(4512609184158823346)
XLA Ops:
  12.9 14.7 all_gather.25
  39.0 65.1 %all-reduce.3.cloned.1.call-done = f32[1024,512]{1,0:T(8,128)} async-done(((f32[1024,512]{1,0:T(8,128)}), f32[1024,512]{1,0:T(8,128)}) %all-reduce.3.cloned.1.call-update) | async-done | bytes 2097168 | tf_op jit(solution)/shard_map/psum | solution.py:50
  108.8 39.4 %all-reduce = (f32[]{:T(128)}, f32[]{:T(128)}, f32[]{:T(128)}, f32[]{:T(128)}, f32[]{:T(128)}) all-reduce(f32[]{:T(128)S(6)} %select_n.20, f32[]{:T(128)S(6)} %mul.139, f32[]{:T(128)S(6)} %mul.141, f32[]{:T(128)S(6)} %mul.148, f32[]{:T(128)S(6)} %mul.152), channel_id=1, replica_groups=mesh['bvec'=4,'row'=2,'col'=4] {'bvec','row','col'}, use_global_device_ids=true, to_apply=%region_4.5 | all-reduce | flops 5 | bytes 40 | tf_op jit(solution)/shard_map/psum | solution.py:56
  156.3 14.8 all-gather.5.cloned.1.call-done
  171.2 1178.3 %while.14 = (s32[]{:T(128)}, f32[1024,512]{1,0:T(8,128)S(1)}, f32[2048,512]{1,0:T(8,128)}, s32[512]{0:T(512)S(1)}, s32[1024]{0:T(1024)S(1)}, /*index=5*/s32[]{:T(128)}, s32[]{:T(128)}) while((s32[]{:T(128)}, f32[1024,512]{1,0:T(8,128)S(1)}, f32[2048,512]{1,0:T(8,128)}, s32[512]{0:T(512)S(1)}, s32[1024]{0:T(1024)S(1)}, ...), condition=%wide.region_16.17_spmd.clone, body=%wide.region_15.16_spmd.clone.sunk | while | flops 12886999040 | bytes 54532272 | solution.py:79
  172.5 152.4 %all-gather.11.cloned.1.call-done = f32[1024,2048]{1,0:T(8,128)} async-done(((f32[1024,512]{1,0:T(8,128)}), f32[1024,2048]{1,0:T(8,128)}) %all-gather.11.cloned.1.call-update) | async-done | bytes 8388624 | tf_op jit(solution)/shard_map/while/body/eval_jaxpr/all_gather | solution.py:75
  324.9 17.2 convert_add_fusion.2
  343.5 149.1 %all-gather.11.cloned.1.call-done = f32[1024,2048]{1,0:T(8,128)} async-done(((f32[1024,512]{1,0:T(8,128)}), f32[1024,2048]{1,0:T(8,128)}) %all-gather.11.cloned.1.call-update) | async-done | bytes 8388624 | tf_op jit(solution)/shard_map/while/body/eval_jaxpr/all_gather | solution.py:75
  492.7 17.2 convert_add_fusion.2
  511.2 149.1 %all-gather.11.cloned.1.call-done = f32[1024,2048]{1,0:T(8,128)} async-done(((f32[1024,512]{1,0:T(8,128)}), f32[1024,2048]{1,0:T(8,128)}) %all-gather.11.cloned.1.call-update) | async-done | bytes 8388624 | tf_op jit(solution)/shard_map/while/body/eval_jaxpr/all_gather | solution.py:75
  660.4 17.2 convert_add_fusion.2
  679.0 149.1 %all-gather.11.cloned.1.call-done = f32[1024,2048]{1,0:T(8,128)} async-done(((f32[1024,512]{1,0:T(8,128)}), f32[1024,2048]{1,0:T(8,128)}) %all-gather.11.cloned.1.call-update) | async-done | bytes 8388624 | tf_op jit(solution)/shard_map/while/body/eval_jaxpr/all_gather | solution.py:75
  828.1 17.2 convert_add_fusion.2
  846.7 149.5 %all-gather.11.cloned.1.call-done = f32[1024,2048]{1,0:T(8,128)} async-done(((f32[1024,512]{1,0:T(8,128)}), f32[1024,2048]{1,0:T(8,128)}) %all-gather.11.cloned.1.call-update) | async-done | bytes 8388624 | tf_op jit(solution)/shard_map/while/body/eval_jaxpr/all_gather | solution.py:75
  996.1 17.2 convert_add_fusion.2
  1014.7 149.5 %all-gather.11.cloned.1.call-done = f32[1024,2048]{1,0:T(8,128)} async-done(((f32[1024,512]{1,0:T(8,128)}), f32[1024,2048]{1,0:T(8,128)}) %all-gather.11.cloned.1.call-update) | async-done | bytes 8388624 | tf_op jit(solution)/shard_map/while/body/eval_jaxpr/all_gather | solution.py:75
  1164.2 17.2 convert_add_fusion.2
  1182.8 149.4 %all-gather.11.cloned.1.call-done = f32[1024,2048]{1,0:T(8,128)} async-done(((f32[1024,512]{1,0:T(8,128)}), f32[1024,2048]{1,0:T(8,128)}) %all-gather.11.cloned.1.call-update) | async-done | bytes 8388624 | tf_op jit(solution)/shard_map/while/body/eval_jaxpr/all_gather | solution.py:75
  1332.2 17.2 convert_add_fusion.2
  1354.2 9.8 all-gather.7.cloned.1.call-done
  1364.0 289.5 %all-gather.9.cloned.1.call-done = f32[1,2,1024,2048]{3,2,1,0:T(8,128)} async-done(((f32[1,2,1024,512]{3,2,1,0:T(8,128)}), f32[1,2,1024,2048]{3,2,1,0:T(8,128)}) %all-gather.9.cloned.1.call-update) | async-done | bytes 16777232 | tf_op jit(solution)/shard_map/all_gather | solution.py:81
  1653.5 57.2 %convolution_bitcast_fusion = f32[2048,512]{0,1:T(8,128)} fusion(f32[2048,512]{1,0:T(8,128)} %all-gather.7.cloned.1.call-done, f32[2048,2048]{1,0:T(8,128)} %bitcast.27), kind=kOutput, calls=%fused_computation.5 | convolution fusion | flops 25769803776 | bytes 25165824 | tf_op jit(solution)/shard_map/dot_general | solution.py:14
  1725.9 21.9 %all_gather.29 = f32[1,2,2048]{1,2,0:T(8,128)S(1)} all-gather(f32[1,2,512]{1,2,0:T(8,128)S(1)} %psum.63), channel_id=1, replica_groups=mesh['bvec'=4,'row'=2,'col'=4] {'col'}, dimensions={2}, use_global_device_ids=true | all-gather | bytes 20480 | tf_op jit(solution)/shard_map/all_gather | solution.py:88
  1748.1 8.2 all_gather.30
  (73 shorter events, 54.7 us)
Async XLA Ops:
  7.2 97.0 %all-reduce.3.cloned.1.call-start = ((), (), s32[]{:S(2)}) async-start(), calls=%async_computation | async-start | bytes 4194304 | tf_op jit(solution)/shard_map/psum | solution.py:50
  7.5 20.2 %copy-start.6 = (f32[6]{0:T(128)S(1)}, f32[6]{0:T(128)}, u32[]{:S(2)}) copy-start(f32[6]{0:T(128)} %param.9) | copy-start | bytes 76
  7.5 20.2 %copy-start.7 = (s32[4]{0:T(128)S(1)}, s32[4]{0:T(128)}, u32[]{:S(2)}) copy-start(s32[4]{0:T(128)} %param.8) | copy-start | bytes 52
  33.5 70.7 %copy-start.5 = (f32[1024,512]{1,0:T(8,128)S(1)}, f32[1024,512]{1,0:T(8,128)}, u32[]{:S(2)}) copy-start(f32[1024,512]{1,0:T(8,128)} %param.11) | copy-start | bytes 6291460
  33.5 137.7 %all-gather.5.cloned.1.call-start = ((), (), s32[]{:S(2)}) async-start(), calls=%async_computation.1 | async-start | bytes 6291456 | tf_op jit(solution)/shard_map/all_gather | solution.py:69
  171.2 153.8 %all-gather.11.cloned.1.call-start = ((), (), s32[]{:S(2)}) async-start(), calls=%async_computation.4 | async-start | bytes 10485760 | tf_op jit(solution)/shard_map/while/body/eval_jaxpr/all_gather | solution.py:75
  342.2 1.3 copy-start
  342.2 150.5 %all-gather.11.cloned.1.call-start = ((), (), s32[]{:S(2)}) async-start(), calls=%async_computation.4 | async-start | bytes 10485760 | tf_op jit(solution)/shard_map/while/body/eval_jaxpr/all_gather | solution.py:75
  509.9 1.3 copy-start
  509.9 150.5 %all-gather.11.cloned.1.call-start = ((), (), s32[]{:S(2)}) async-start(), calls=%async_computation.4 | async-start | bytes 10485760 | tf_op jit(solution)/shard_map/while/body/eval_jaxpr/all_gather | solution.py:75
  677.6 1.3 copy-start
  677.6 150.5 %all-gather.11.cloned.1.call-start = ((), (), s32[]{:S(2)}) async-start(), calls=%async_computation.4 | async-start | bytes 10485760 | tf_op jit(solution)/shard_map/while/body/eval_jaxpr/all_gather | solution.py:75
  845.3 1.3 copy-start
  845.3 150.8 %all-gather.11.cloned.1.call-start = ((), (), s32[]{:S(2)}) async-start(), calls=%async_computation.4 | async-start | bytes 10485760 | tf_op jit(solution)/shard_map/while/body/eval_jaxpr/all_gather | solution.py:75
  1013.4 1.3 copy-start
  1013.4 150.8 %all-gather.11.cloned.1.call-start = ((), (), s32[]{:S(2)}) async-start(), calls=%async_computation.4 | async-start | bytes 10485760 | tf_op jit(solution)/shard_map/while/body/eval_jaxpr/all_gather | solution.py:75
  1181.4 1.3 copy-start
  1181.4 150.8 %all-gather.11.cloned.1.call-start = ((), (), s32[]{:S(2)}) async-start(), calls=%async_computation.4 | async-start | bytes 10485760 | tf_op jit(solution)/shard_map/while/body/eval_jaxpr/all_gather | solution.py:75
  1349.4 1.3 copy-start.1
  1349.5 14.5 all-gather.7.cloned.1.call-start
  1350.8 1.6 copy-start.2
  1350.8 302.7 %all-gather.9.cloned.1.call-start = ((), (), s32[]{:S(2)}) async-start(), calls=%async_computation.3 | async-start | bytes 20971520 | tf_op jit(solution)/shard_map/all_gather | solution.py:81
  1710.7 6.7 copy-start.4
  1721.7 36.0 %copy-start.3 = (f32[1024,512]{1,0:T(8,128)S(1)}, f32[1024,512]{1,0:T(8,128)}, u32[]{:S(2)}) copy-start(f32[1024,512]{1,0:T(8,128)} %all-reduce.3.cloned.1.call-done) | copy-start | bytes 6291460
  (1 other events, 1.3 us)
Sparse Core Ops, SparseCore 0:
  33.6 70.4 all-reduce.2
  156.5 14.6 all-gather.4
  174.1 150.7 all-gather.10
  344.8 147.7 all-gather.10
  512.5 147.7 all-gather.10
  680.3 147.7 all-gather.10
  848.3 147.7 all-gather.10
  1016.4 147.7 all-gather.10
  1184.4 147.7 all-gather.10
  1352.1 11.8 all-gather.6
  1365.5 287.9 all-gather.8
where the time goes:
time: 1770 us
  waiting for transfers between devices  1430 us (81%)
  matrix products  178 us (10%)
  blocking collectives  91 us (5%)
  other arithmetic  24.3 us (1%)
  between operations  22.9 us (1%)
  local copies, waits for them, and re-layouts  22.4 us (1%)
    all_gather x7, waiting for transfers between devices, horner_step(): folded = accumulate(lax.all_gather(current, 'col', axis=1, tiled=True))  1050 us
    all_gather x1, waiting for transfers between devices, shards(): section = lax.all_gather(m_matrices, 'col', axis=3, tiled=True)  290 us
    dot_general x8, matrix products, product(): jnp.dot(left, right, precision=HIGHEST, preferred_element_type=jnp.float32)  178 us
    psum x1, waiting for transfers between devices, shards(): gradient = lax.psum(grad_part, 'bvec')  65.1 us
    psum x1, blocking collectives, shards(): lax.psum((spread_term, grad_square, prev_square, cross_term, dir_square),...  39.4 us
  transfers between devices with their start and end apart: 11, of which 11 were waited for; matrix products, arithmetic and copies ran while one was open for 0% of the time, Pallas kernels for 0%

commit v1 on v0

v1 whole, which is shorter than its diff:
```python
import jax
import jax.numpy as jnp
from jax import lax
from jax.sharding import PartitionSpec as P

TAYLOR = 8
STEP_SCALE = 1.75
HIGH = lax.Precision.HIGH
ALL = ("bvec", "row", "col")


def product(left, right):
    return jnp.dot(left, right, precision=HIGH, preferred_element_type=jnp.float32)


def lookup_weights(bvec_index, weight_table):
    table_slots = jnp.arange(weight_table.shape[0], dtype=jnp.int32)
    return jnp.sum(
        jnp.where(table_slots[None, :] == bvec_index[:, None], weight_table[None, :], 0.0), axis=1
    )


def shards(m_matrices, bvec_index, weight_table, grad_prev, dir_prev):
    per_group = m_matrices.shape[0]
    local_rows = m_matrices.shape[2]
    local_cols = m_matrices.shape[3]
    groups, n_row, n_col = (lax.axis_size(a) for a in ALL)
    devices = groups * n_row * n_col
    order = local_rows * n_row
    group = lax.axis_index("bvec")
    row, col = lax.axis_index("row"), lax.axis_index("col")
    row_start = row * local_rows
    col_start = col * local_cols
    weight_all = lookup_weights(bvec_index, weight_table)
    weight_own = lax.dynamic_slice_in_dim(weight_all, group * per_group, per_group)
    row_ids = row_start + jnp.arange(local_rows, dtype=jnp.int32)
    col_ids = col_start + jnp.arange(local_cols, dtype=jnp.int32)
    on_diag = row_ids[:, None] == col_ids[None, :]
    own_diag = jnp.sum(jnp.where(on_diag, m_matrices, 0.0), axis=2)
    diag_parts = lax.all_gather(own_diag, ("row", "col"))
    diag_parts = diag_parts.reshape(n_row, n_col, per_group, 2, local_cols).sum(axis=0)
    diagonal = diag_parts.transpose(1, 2, 0, 3).reshape(per_group, 2, order)
    row_diag = lax.dynamic_slice_in_dim(diagonal, row_start, local_rows, 2)
    col_diag = lax.dynamic_slice_in_dim(diagonal, col_start, local_cols, 2)
    spread_own = (
        jnp.sum(weight_own[:, None] * (1.0 - diagonal[:, 0] ** 2 - diagonal[:, 1] ** 2)) / order
    )
    spread_term = jnp.where((row == 0) & (col == 0), spread_own, 0.0)
    differ = row_diag[:, :, :, None] - col_diag[:, :, None, :]
    weighted = 2.0 * weight_own[:, None, None] * jnp.sum(m_matrices * differ, axis=1)
    grad_part = jnp.sum(weighted, axis=0)
    grad_piece = lax.psum_scatter(grad_part, "bvec", scatter_dimension=0, tiled=True)
    piece_rows = local_rows // groups
    prev_piece = lax.dynamic_slice_in_dim(grad_prev, group * piece_rows, piece_rows, 0)
    dir_piece = lax.dynamic_slice_in_dim(dir_prev, group * piece_rows, piece_rows, 0)
    sums = jnp.stack(
        [
            spread_term,
            jnp.sum(grad_piece * grad_piece),
            jnp.sum(prev_piece * prev_piece),
            jnp.sum(grad_piece * dir_piece),
            jnp.sum(dir_piece * dir_piece),
        ]
    )
    totals = jnp.sum(lax.all_gather(sums, ALL), axis=0)
    spread = totals[0]
    beta_factor = totals[1] / (1.0 + totals[2])
    dir_norm = jnp.maximum(
        totals[1] - 2.0 * beta_factor * totals[3] + beta_factor * beta_factor * totals[4], 0.0
    )
    scale = STEP_SCALE / jnp.sqrt(1.0 + dir_norm / order)
    x_piece = scale * (beta_factor * dir_piece - grad_piece)
    pieces = lax.all_gather(x_piece, ALL)
    grad_in, _ = lax.optimization_barrier((grad_piece, pieces[0, 0, 0]))
    gradient = lax.all_gather(grad_in, "bvec", axis=0, tiled=True)
    direction = beta_factor * dir_prev - gradient

    whole = pieces.reshape(groups, n_row, n_col, piece_rows, local_cols)
    generator = whole.transpose(1, 0, 3, 2, 4).reshape(order, order)
    slab = order // devices
    me = (group * n_row + row) * n_col + col
    slab_ids = me * slab + jnp.arange(slab, dtype=jnp.int32)
    eye_slab = (slab_ids[:, None] == jnp.arange(order, dtype=jnp.int32)[None, :]).astype(jnp.float32)
    iterate = eye_slab + lax.dynamic_slice_in_dim(generator, me * slab, slab, 0) / TAYLOR
    for divisor in range(TAYLOR - 1, 0, -1):
        iterate = eye_slab + product(iterate, generator) / divisor
    expmap = lax.all_gather(iterate, ALL, axis=0, tiled=True)
    exp_rows = lax.dynamic_slice_in_dim(expmap, row_start, local_rows, 0)
    exp_cols = lax.dynamic_slice_in_dim(expmap, col_start, local_cols, 0)
    flat = m_matrices.reshape(-1, local_cols)
    rotated = product(flat, exp_cols).reshape(per_group, 2, local_rows, order)
    trial_part = jnp.sum(exp_rows[None, None] * rotated, axis=2)
    trial_parts = lax.all_gather(trial_part, ALL)
    trial_diag = trial_parts.reshape(groups, n_row * n_col, per_group, 2, order).sum(axis=1)
    trial_diag = trial_diag.reshape(groups * per_group, 2, order)
    trial_spread = (
        jnp.sum(weight_all[:, None] * (1.0 - trial_diag[:, 0] ** 2 - trial_diag[:, 1] ** 2)) / order
    )
    return (spread, trial_spread, gradient, direction, trial_diag)


def solution(mesh):
    placed = (P("bvec", None, "row", "col"), P(), P(), P("row", "col"), P("row", "col"))
    return jax.shard_map(
        shards,
        mesh=mesh,
        in_specs=placed,
        out_specs=(P(), P(), P("row", "col"), P("row", "col"), P()),
        check_vma=False,
    )
```

time: 1770 us -> 542 us (0.31)
  waiting for transfers between devices: 1430 us -> 257 us
  matrix products: 178 us -> 61.7 us
  blocking collectives: 91 us -> 134 us
    all_gather x10 -> x3, waiting for transfers between devices: 1360 us -> 224 us  [the longest x1 114 us: shards(): pieces = lax.all_gather(x_piece, ALL)]
    dot_general x8, matrix products: 178 us -> 61.7 us  [product(): jnp.dot(left, right, precision=HIGH, preferred_element_type=jnp.float32)]
    psum x1 -> x0, waiting for transfers between devices: 65.1 us -> none  [shards(): gradient = lax.psum(grad_part, 'bvec')]
    all_gather x3 -> x2, blocking collectives: 44.8 us -> 95.2 us  [the longest x1 69.9 us: shards(): trial_parts = lax.all_gather(trial_part, ALL)]
    psum x3 -> x0, blocking collectives: 46.1 us -> none  [the longest x1 39.4 us: shards(): lax.psum((spread_term, grad_square, prev_square, cross_term, dir_square),...]
    unnamed x0 -> x1, blocking collectives: none -> 39.3 us
    reduce_scatter x0 -> x1, waiting for transfers between devices: none -> 32.9 us  [shards(): lax.psum_scatter(grad_part, 'bvec', scatter_dimension=0, tiled=True)]
  transfers between devices with their start and end apart: 11 -> 4, of which waited for: 11 -> 3; matrix products, arithmetic and copies ran while one was open for 0% -> 14% of each run, Pallas kernels for 0% -> 0%
where the time goes in v1:
time: 542 us; the launch traced here: 537 us
  waiting for transfers between devices  257 us (47%)
  blocking collectives  134 us (25%)
  matrix products  61.7 us (11%)
  local copies, waits for them, and re-layouts  35.4 us (7%)
  other arithmetic  27 us (5%)
  between operations  20.6 us (4%)
    all_gather x1, waiting for transfers between devices, shards(): pieces = lax.all_gather(x_piece, ALL)  114 us
    all_gather x1, waiting for transfers between devices, shards(): expmap = lax.all_gather(iterate, ALL, axis=0, tiled=True)  109 us
    all_gather x1, blocking collectives, shards(): trial_parts = lax.all_gather(trial_part, ALL)  69.9 us
    dot_general x8, matrix products, product(): jnp.dot(left, right, precision=HIGH, preferred_element_type=jnp.float32)  61.7 us
    unnamed x1, blocking collectives  39.3 us
    reduce_scatter x1, waiting for transfers between devices, shards(): lax.psum_scatter(grad_part, 'bvec', scatter_dimension=0, tiled=True)  32.9 us
    all_gather x1, blocking collectives, shards(): diag_parts = lax.all_gather(own_diag, ('row', 'col'))  25.2 us
    reshape x1, local copies, waits for them, and re-layouts, shards(): whole = pieces.reshape(groups, n_row, n_col, piece_rows, local_cols)  19 us
  transfers between devices with their start and end apart: 4, of which 3 were waited for; matrix products, arithmetic and copies ran while one was open for 14% of the time, Pallas kernels for 0%

profile of v1, /device:TPU:0, one launch (start us, length us, event | category | flops | bytes accessed | tf_op | source)
XLA Modules:
  0.0 536.7 jit_solution(14850138140524838844)
XLA Ops:
  7.6 2.9 select_reduce_fusion
  10.6 25.2 %all-gather.4 = f32[8,2,512]{2,1,0:T(2,128)S(1)} all-gather(f32[1,2,512]{2,1,0:T(2,128)S(1)} %bitcast.69), channel_id=2, replica_groups=mesh['bvec'=4,'row'=2,'col'=4] {'row','col'}, dimensions={0}, use_global_device_ids=true | all-gather | bytes 36864 | tf_op jit(solution)/shard_map/all_gather | solution.py:40
  37.3 2.8 multiply_reduce_fusion.1
  46.1 32.9 %reduce-scatter.2.cloned.1.call-done = f32[256,512]{1,0:T(8,128)} async-done(((f32[1024,512]{1,0:T(8,128)}), f32[256,512]{1,0:T(8,128)}) %reduce-scatter.2.cloned.1.call-update) | async-done | bytes 524304 | tf_op jit(solution)/shard_map/reduce_scatter | solution.py:52
  79.1 1.8 multiply_reduce_fusion.2
  80.9 2.7 stack.23
  83.8 39.3 %all-reduce = f32[160]{0:T(256)S(1)} all-reduce(f32[160]{0:T(256)S(1)} %dynamic-update-slice), channel_id=3, replica_groups=mesh['bvec'=4,'row'=2,'col'=4] {'bvec','row','col'}, use_global_device_ids=true, to_apply=%add | all-reduce | flops 160 | bytes 1280
  127.0 1.9 subtract_multiply_fusion
  129.8 114.4 %all-gather.14.cloned.1.call-done = f32[8192,512]{1,0:T(8,128)} async-done(((f32[256,512]{1,0:T(8,128)}), f32[8192,512]{1,0:T(8,128)}) %all-gather.14.cloned.1.call-update) | async-done | bytes 16777232 | tf_op jit(solution)/shard_map/all_gather | solution.py:73
  244.2 19.0 %copy.14 = f32[4,2,4,256,512]{4,2,3,0,1:T(4,128)S(1)} copy(f32[4,2,4,256,512]{4,3,2,1,0:T(8,128)} %bitcast.61) | data formatting | bytes 33554432 | tf_op jit(solution)/shard_map/reshape | solution.py:78
  263.2 6.3 %copy.16 = f32[256,8,4,512]{3,1,2,0:T(8,128)S(1)} copy(f32[256,8,4,512]{3,2,1,0:T(4,128)S(1)} %bitcast.60) | data formatting | bytes 33554432
  269.6 6.0 %fusion.7 = f32[64,2048]{1,0:T(8,128)S(1)} fusion(f32[2048,2048]{1,0:T(8,128)S(1)} %bitcast.53, s32[]{:T(128)S(6)} %select_n.37, s32[64]{0:T(128)S(1)} %iota_add_fusion.2), kind=kOutput, calls=%fused_computation.17 | convolution fusion | flops 1611661312 | bytes 17826820 | tf_op jit(solution)/shard_map/dot_general | solution.py:13
  275.6 6.0 %fusion.6 = f32[64,2048]{1,0:T(8,128)S(1)} fusion(f32[64,2048]{1,0:T(8,128)S(1)} %fusion.7, f32[2048,2048]{1,0:T(8,128)S(1)} %bitcast.54, s32[64]{0:T(128)S(1)} %iota_add_fusion.2), kind=kOutput, calls=%fused_computation.15 | convolution fusion | flops 1611137024 | bytes 17826048 | tf_op jit(solution)/shard_map/dot_general | solution.py:13
  281.6 6.2 %fusion.5 = f32[64,2048]{1,0:T(8,128)S(1)} fusion(f32[64,2048]{1,0:T(8,128)S(1)} %fusion.6, f32[2048,2048]{1,0:T(8,128)S(1)} %bitcast.55, s32[64]{0:T(128)S(1)} %iota_add_fusion.2), kind=kOutput, calls=%fused_computation.13 | convolution fusion | flops 1611137024 | bytes 17826048 | tf_op jit(solution)/shard_map/dot_general | solution.py:13
  287.8 6.0 %fusion.4 = f32[64,2048]{1,0:T(8,128)S(1)} fusion(f32[64,2048]{1,0:T(8,128)S(1)} %fusion.5, f32[2048,2048]{1,0:T(8,128)S(1)} %bitcast.56, s32[64]{0:T(128)S(1)} %iota_add_fusion.2), kind=kOutput, calls=%fused_computation.11 | convolution fusion | flops 1611137024 | bytes 17826048 | tf_op jit(solution)/shard_map/dot_general | solution.py:13
  293.7 6.0 %fusion.3 = f32[64,2048]{1,0:T(8,128)S(1)} fusion(f32[64,2048]{1,0:T(8,128)S(1)} %fusion.4, f32[2048,2048]{1,0:T(8,128)S(1)} %bitcast.57, s32[64]{0:T(128)S(1)} %iota_add_fusion.2), kind=kOutput, calls=%fused_computation.9 | convolution fusion | flops 1611137024 | bytes 17826048 | tf_op jit(solution)/shard_map/dot_general | solution.py:13
  299.7 6.4 %fusion.2 = f32[64,2048]{1,0:T(8,128)S(1)} fusion(f32[64,2048]{1,0:T(8,128)S(1)} %fusion.3, f32[2048,2048]{1,0:T(8,128)S(1)} %bitcast.58, s32[64]{0:T(128)S(1)} %iota_add_fusion.2), kind=kOutput, calls=%fused_computation.7 | convolution fusion | flops 1611137024 | bytes 17826048 | tf_op jit(solution)/shard_map/dot_general | solution.py:13
  306.1 6.8 %convolution_add_fusion = f32[64,2048]{1,0:T(8,128)} fusion(f32[64,2048]{1,0:T(8,128)S(1)} %fusion.2, f32[2048,2048]{1,0:T(8,128)S(1)} %bitcast.59, s32[64]{0:T(128)S(1)} %iota_add_fusion.2), kind=kOutput, calls=%fused_computation.5 | convolution fusion | flops 1611005952 | bytes 17826048 | tf_op jit(solution)/shard_map/dot_general | solution.py:13
  312.9 3.4 multiply_subtract_fusion
  316.3 109.3 %all-gather.10.cloned.1.call-done = f32[2048,2048]{1,0:T(8,128)} async-done(((f32[64,2048]{1,0:T(8,128)}), f32[2048,2048]{1,0:T(8,128)}) %all-gather.10.cloned.1.call-update) | async-done | bytes 16777232 | tf_op jit(solution)/shard_map/all_gather | solution.py:87
  425.6 4.1 constant_dynamic-slice_fusion
  430.2 18.4 %fusion = f32[2048,2048]{0,1:T(8,128)} fusion(f32[2048,512]{1,0:T(8,128)S(1)} %bitcast.63, f32[2048,2048]{1,0:T(8,128)} %all-gather.10.cloned.1.call-done, s32[]{:T(128)S(6)} %select_n.35), kind=kOutput, calls=%fused_computation.1 | convolution fusion | flops 12884901888 | bytes 25165828 | tf_op jit(solution)/shard_map/dot_general | solution.py:13
  448.6 7.4 %multiply_reduce_fusion = f32[2,2048]{1,0:T(2,128)S(1)} fusion(f32[1,2,1024,2048]{3,2,1,0:T(8,128)} %bitcast.62, f32[1024,2048]{1,0:T(8,128)S(1)} %constant_dynamic-slice_fusion), kind=kLoop, calls=%fused_computation | loop fusion | flops 8384512 | bytes 25182208 | tf_op jit(solution)/shard_map/reduce_sum | solution.py:92
  456.0 69.9 %all-gather.5 = f32[32,2,2048]{2,1,0:T(2,128)S(1)} all-gather(f32[1,2,2048]{2,1,0:T(2,128)S(1)} %bitcast.68), channel_id=5, replica_groups=mesh['bvec'=4,'row'=2,'col'=4] {'bvec','row','col'}, dimensions={0}, use_global_device_ids=true | all-gather | bytes 540672 | tf_op jit(solution)/shard_map/all_gather | solution.py:93
  (38 shorter events, 10.9 us)
Async XLA Ops:
  7.2 71.9 %reduce-scatter.2.cloned.1.call-start = ((), (), s32[]{:S(2)}) async-start(), calls=%async_computation.1 | async-start | bytes 2621440 | tf_op jit(solution)/shard_map/reduce_scatter | solution.py:52
  7.6 71.5 %copy-start.2 = (f32[1024,512]{1,0:T(8,128)S(1)}, f32[1024,512]{1,0:T(8,128)}, u32[]{:S(2)}) copy-start(f32[1024,512]{1,0:T(8,128)} %param.9) | copy-start | bytes 6291460
  42.4 201.9 %all-gather.14.cloned.1.call-start = ((), (), s32[]{:S(2)}) async-start(), calls=%async_computation.4 | async-start | bytes 17301504 | tf_op jit(solution)/shard_map/all_gather | solution.py:73
  129.0 183.9 %all-gather.12.cloned.1.call-start = ((), (), s32[]{:S(2)}) async-start(), calls=%async_computation.3 | async-start | bytes 2621440 | tf_op jit(solution)/shard_map/all_gather | solution.py:75
  129.7 295.9 %all-gather.10.cloned.1.call-start = ((), (), s32[]{:S(2)}) async-start(), calls=%async_computation.2 | async-start | bytes 17301504 | tf_op jit(solution)/shard_map/all_gather | solution.py:87
  425.6 4.6 copy-start
  448.6 78.9 %copy-start.1 = (f32[1024,512]{1,0:T(8,128)S(1)}, f32[1024,512]{1,0:T(8,128)}, u32[]{:S(2)}) copy-start(f32[1024,512]{1,0:T(8,128)} %all-gather.12.cloned.1.call-done) | copy-start | bytes 6291460
  526.1 2.7 copy-start.3
Sparse Core Ops, SparseCore 0:
  42.5 36.5 reduce-scatter.1
  129.1 115.0 all-gather.13
  246.1 33.3 all-gather.11
  313.0 112.5 all-gather.9

commit v2 on v1

--- a/solution.py
+++ b/solution.py
@@ -1,6 +1,8 @@
 import jax
 import jax.numpy as jnp
 from jax import lax
+from jax.experimental import pallas as pl
+from jax.experimental.pallas import tpu as pltpu
 from jax.sharding import PartitionSpec as P
 
 TAYLOR = 8
@@ -11,6 +13,222 @@
 
 def product(left, right):
     return jnp.dot(left, right, precision=HIGH, preferred_element_type=jnp.float32)
+
+
+def member(position, axes, sizes):
+    where = {}
+    for axis, size in zip(reversed(axes), reversed(sizes)):
+        where[axis] = lax.rem(position, size)
+        position = lax.div(position, size)
+    return where
+
+
+def small_gather(block, axes, collective_id):
+    sizes = tuple(lax.axis_size(axis) for axis in axes)
+    count = 1
+    for size in sizes:
+        count *= size
+    if count > 32:
+        return lax.all_gather(block, axes)
+
+    def kernel(block_ref, out_ref, send_sem, recv_sem, local_sem):
+        me = lax.axis_index(axes[0])
+        for axis, size in zip(axes[1:], sizes[1:]):
+            me = me * size + lax.axis_index(axis)
+        barrier = pltpu.get_barrier_semaphore()
+
+        def peer(step):
+            return member(lax.rem(me + step, count), axes, sizes)
+
+        def greet(step, carry):
+            pl.semaphore_signal(
+                barrier, inc=1, device_id=peer(step), device_id_type=pl.DeviceIdType.MESH
+            )
+            return carry
+
+        def copy(step):
+            return pltpu.make_async_remote_copy(
+                src_ref=block_ref,
+                dst_ref=out_ref.at[me],
+                send_sem=send_sem.at[step],
+                recv_sem=recv_sem.at[step],
+                device_id=peer(step),
+                device_id_type=pl.DeviceIdType.MESH,
+            )
+
+        def start(step, carry):
+            copy(step).start()
+            return carry
+
+        def finish(step, carry):
+            copy(step).wait()
+            return carry
+
+        own = pltpu.make_async_copy(block_ref, out_ref.at[me], local_sem)
+        own.start()
+        lax.fori_loop(1, count, greet, 0)
+        pl.semaphore_wait(barrier, count - 1)
+        lax.fori_loop(1, count, start, 0)
+        lax.fori_loop(1, count, finish, 0)
+        own.wait()
+
+    return pl.pallas_call(
+        kernel,
+        out_shape=jax.ShapeDtypeStruct((count,) + block.shape, block.dtype),
+        in_specs=[pl.BlockSpec(memory_space=pltpu.VMEM)],
+        out_specs=pl.BlockSpec(memory_space=pltpu.VMEM),
+        scratch_shapes=[
+            pltpu.SemaphoreType.DMA((count,)),
+            pltpu.SemaphoreType.DMA((count,)),
+            pltpu.SemaphoreType.DMA,
+        ],
+        compiler_params=pltpu.CompilerParams(collective_id=collective_id, has_side_effects=True),
+    )(block)
+
+
+def wide_gather(piece, shape, place, band, collective_id):
+    quarter = piece.shape[0] // 4
+    first, second = (0, 2 * quarter), (2 * quarter, 2 * quarter)
+    quarters = [(i * quarter, quarter) for i in range(4)]
+
+    def kernel(piece_ref, out_ref, send_sem, recv_sem, local_sem):
+        g, r, c = (lax.axis_index(a) for a in ALL)
+        gx, gy = g + 1 - 2 * lax.rem(g, 2), lax.rem(g + 2, 4)
+        gd = lax.rem(gx + 2, 4)
+        cp, cm, c2 = lax.rem(c + 1, 4), lax.rem(c + 3, 4), lax.rem(c + 2, 4)
+        to_x, to_y = {"bvec": gx}, {"bvec": gy}
+        to_p, to_m = {"col": cp}, {"col": cm}
+        to_core = {"row": 1 - r}
+        started = []
+
+        def send(source, target, peer):
+            k = len(started)
+            copy = pltpu.make_async_remote_copy(
+                src_ref=source,
+                dst_ref=target,
+                send_sem=send_sem.at[k],
+                recv_sem=recv_sem.at[k],
+                device_id=peer,
+                device_id_type=pl.DeviceIdType.MESH,
+            )
+            copy.start()
+            started.append(copy)
+            return copy
+
+        def own(part, peer):
+            return send(piece_ref.at[pl.ds(*part)], place(out_ref, g, r, c, part), peer)
+
+        def pass_on(gg, cc, part, peer):
+            spot = place(out_ref, gg, r, cc, part)
+            return send(spot, spot, peer)
+
+        def share(gg, part):
+            spot = band(out_ref, gg, r, part)
+            return send(spot, spot, to_core)
+
+        barrier = pltpu.get_barrier_semaphore()
+        for peer in (to_x, to_y, to_p, to_m, to_core):
+            pl.semaphore_signal(barrier, inc=1, device_id=peer, device_id_type=pl.DeviceIdType.MESH)
+        pl.semaphore_wait(barrier, 5)
+        a_p, a_m = own(first, to_p), own(first, to_m)
+        b_x, b_y = own(second, to_x), own(second, to_y)
+        ax, ay, bp, bm = {}, {}, {}, {}
+        ax[0], ay[0] = own(first, to_x), own(first, to_y)
+        bp[0], bm[0] = own(second, to_p), own(second, to_m)
+        local = pltpu.make_async_copy(
+            piece_ref, place(out_ref, g, r, c, (0, 4 * quarter)), local_sem
+        )
+        local.start()
+        a_p.wait_recv()
+        relay_p = pass_on(g, cm, quarters[0], to_p)
+        b_x.wait_recv()
+        relay_y = pass_on(gx, c, quarters[2], to_y)
+        a_m.wait_recv()
+        relay_m = pass_on(g, cp, quarters[1], to_m)
+        b_y.wait_recv()
+        relay_x = pass_on(gy, c, quarters[3], to_x)
+        ax[1], ay[1] = pass_on(g, cm, first, to_x), pass_on(g, cm, first, to_y)
+        bp[1], bm[1] = pass_on(gx, c, second, to_p), pass_on(gx, c, second, to_m)
+        ax[2], ay[2] = pass_on(g, cp, first, to_x), pass_on(g, cp, first, to_y)
+        bp[2], bm[2] = pass_on(gy, c, second, to_p), pass_on(gy, c, second, to_m)
+        relay_p.wait_recv()
+        relay_m.wait_recv()
+        ax[3], ay[3] = pass_on(g, c2, first, to_x), pass_on(g, c2, first, to_y)
+        relay_y.wait_recv()
+        relay_x.wait_recv()
+        bp[3], bm[3] = pass_on(gd, c, second, to_p), pass_on(gd, c, second, to_m)
+        local.wait()
+        last = [share(g, first)]
+        columns, groups = (c, cm, cp, c2), (g, gx, gy, gd)
+        for k in range(4):
+            ax[k].wait_recv()
+            last.append(pass_on(gx, columns[k], quarters[0], to_y))
+            ay[k].wait_recv()
+            last.append(pass_on(gy, columns[k], quarters[1], to_x))
+            bp[k].wait_recv()
+            last.append(pass_on(groups[k], cm, quarters[2], to_p))
+            bm[k].wait_recv()
+            last.append(pass_on(groups[k], cp, quarters[3], to_m))
+        last.append(share(gx, first))
+        last.append(share(gy, first))
+        for k in range(4):
+            for copy in last[1 + 4 * k : 5 + 4 * k]:
+                copy.wait_recv()
+            last.append(share(groups[k], second))
+        last.append(share(gd, first))
+        last[0].wait_recv()
+        for copy in last[17:]:
+            copy.wait_recv()
+        for copy in started:
+            copy.wait_send()
+
+    return pl.pallas_call(
+        kernel,
+        out_shape=jax.ShapeDtypeStruct(shape, piece.dtype),
+        in_specs=[pl.BlockSpec(memory_space=pl.ANY)],
+        out_specs=pl.BlockSpec(memory_space=pl.ANY),
+        scratch_shapes=[
+            pltpu.SemaphoreType.DMA((64,)),
+            pltpu.SemaphoreType.DMA((64,)),
+            pltpu.SemaphoreType.DMA,
+        ],
+        compiler_params=pltpu.CompilerParams(collective_id=collective_id, has_side_effects=True),
+    )(piece)
+
+
+def gather_generator(x_piece):
+    groups, n_row, n_col = (lax.axis_size(a) for a in ALL)
+    rows, cols = x_piece.shape
+    order = cols * n_col
+    if (groups, n_row, n_col) != (4, 2, 4):
+        whole = lax.all_gather(x_piece, ALL).reshape(groups, n_row, n_col, rows, cols)
+        return whole.transpose(1, 0, 3, 2, 4).reshape(order, order)
+
+    def lines(g, r, part):
+        return pl.ds(pl.multiple_of((r * groups + g) * rows + part[0], 8), part[1])
+
+    def place(ref, g, r, c, part):
+        return ref.at[lines(g, r, part), pl.ds(pl.multiple_of(c * cols, 128), cols)]
+
+    def band(ref, g, r, part):
+        return ref.at[lines(g, r, part)]
+
+    return wide_gather(x_piece, (order, order), place, band, 3)
+
+
+def gather_expmap(slab):
+    groups, n_row, n_col = (lax.axis_size(a) for a in ALL)
+    rows, order = slab.shape
+    if (groups, n_row, n_col) != (4, 2, 4):
+        return lax.all_gather(slab, ALL, axis=0, tiled=True)
+
+    def place(ref, g, r, c, part):
+        return ref.at[(g * n_row + r) * n_col + c, pl.ds(*part)]
+
+    def band(ref, g, r, part):
+        return ref.at[pl.ds((g * n_row + r) * n_col, n_col), pl.ds(*part)]
+
+    return wide_gather(slab, (order // rows, rows, order), place, band, 4).reshape(order, order)
 
 
 def lookup_weights(bvec_index, weight_table):
@@ -37,7 +255,7 @@
     col_ids = col_start + jnp.arange(local_cols, dtype=jnp.int32)
     on_diag = row_ids[:, None] == col_ids[None, :]
     own_diag = jnp.sum(jnp.where(on_diag, m_matrices, 0.0), axis=2)
-    diag_parts = lax.all_gather(own_diag, ("row", "col"))
+    diag_parts = small_gather(own_diag.reshape(-1, 128), ("row", "col"), 0)
     diag_parts = diag_parts.reshape(n_row, n_col, per_group, 2, local_cols).sum(axis=0)
     diagonal = diag_parts.transpose(1, 2, 0, 3).reshape(per_group, 2, order)
     row_diag = lax.dynamic_slice_in_dim(diagonal, row_start, local_rows, 2)
@@ -62,7 +280,8 @@
             jnp.sum(dir_piece * dir_piece),
         ]
     )
-    totals = jnp.sum(lax.all_gather(sums, ALL), axis=0)
+    sums = jnp.pad(sums[None, :], ((0, 7), (0, 128 - sums.shape[0])))
+    totals = jnp.sum(small_gather(sums, ALL, 1), axis=0)[0]
     spread = totals[0]
     beta_factor = totals[1] / (1.0 + totals[2])
     dir_norm = jnp.maximum(
@@ -70,13 +289,11 @@
     )
     scale = STEP_SCALE / jnp.sqrt(1.0 + dir_norm / order)
     x_piece = scale * (beta_factor * dir_piece - grad_piece)
-    pieces = lax.all_gather(x_piece, ALL)
-    grad_in, _ = lax.optimization_barrier((grad_piece, pieces[0, 0, 0]))
+    generator = gather_generator(x_piece)
+    grad_in, _ = lax.optimization_barrier((grad_piece, generator[0, 0]))
     gradient = lax.all_gather(grad_in, "bvec", axis=0, tiled=True)
     direction = beta_factor * dir_prev - gradient
 
-    whole = pieces.reshape(groups, n_row, n_col, piece_rows, local_cols)
-    generator = whole.transpose(1, 0, 3, 2, 4).reshape(order, order)
     slab = order // devices
     me = (group * n_row + row) * n_col + col
     slab_ids = me * slab + jnp.arange(slab, dtype=jnp.int32)
@@ -84,13 +301,13 @@
     iterate = eye_slab + lax.dynamic_slice_in_dim(generator, me * slab, slab, 0) / TAYLOR
     for divisor in range(TAYLOR - 1, 0, -1):
         iterate = eye_slab + product(iterate, generator) / divisor
-    expmap = lax.all_gather(iterate, ALL, axis=0, tiled=True)
+    expmap = gather_expmap(iterate)
     exp_rows = lax.dynamic_slice_in_dim(expmap, row_start, local_rows, 0)
     exp_cols = lax.dynamic_slice_in_dim(expmap, col_start, local_cols, 0)
     flat = m_matrices.reshape(-1, local_cols)
     rotated = product(flat, exp_cols).reshape(per_group, 2, local_rows, order)
     trial_part = jnp.sum(exp_rows[None, None] * rotated, axis=2)
-    trial_parts = lax.all_gather(trial_part, ALL)
+    trial_parts = small_gather(trial_part.reshape(-1, 128), ALL, 2)
     trial_diag = trial_parts.reshape(groups, n_row * n_col, per_group, 2, order).sum(axis=1)
     trial_diag = trial_diag.reshape(groups * per_group, 2, order)
     trial_spread = (

time: 542 us -> 397 us (0.73)
  Pallas kernels: 0 us -> 228 us
  waiting for transfers between devices: 257 us -> 32.4 us
  blocking collectives: 134 us -> 0 us
  local copies, waits for them, and re-layouts: 35.4 us -> 16.7 us
    pallas_call x0 -> x5, Pallas kernels: none -> 228 us  [the longest x2 188 us: wide_gather(): pl.pallas_call(kernel, out_shape=jax.ShapeDtypeStruct(shape, piece.dtype)...]
    all_gather x2 -> x0, waiting for transfers between devices: 224 us -> none  [the longest x1 114 us: shards(): pieces = lax.all_gather(x_piece, ALL)]
    all_gather x2 -> x0, blocking collectives: 95.2 us -> none  [the longest x1 69.9 us: shards(): trial_parts = lax.all_gather(trial_part, ALL)]
    unnamed x1 -> x0, blocking collectives: 39.3 us -> none
    reshape x1 -> x4, local copies, waits for them, and re-layouts: 19 us -> 3.31 us  [the longest x1 1.31 us: shards(): trial_parts.reshape(groups, n_row * n_col, per_group, 2, order).sum(axis=1)]
  transfers between devices with their start and end apart: 4 -> 2, of which waited for: 3 -> 1; matrix products, arithmetic and copies ran while one was open for 14% -> 9% of each run, Pallas kernels for 0% -> 5%
where the time goes in v2:
time: 397 us; the launch traced here: 391 us
  Pallas kernels  228 us (57%)
  matrix products  64.7 us (16%)
  waiting for transfers between devices  32.4 us (8%)
  other arithmetic  28.1 us (7%)
  between operations  21.1 us (5%)
  local copies, waits for them, and re-layouts  16.7 us (4%)
    pallas_call x2, Pallas kernels, wide_gather(): pl.pallas_call(kernel, out_shape=jax.ShapeDtypeStruct(shape, piece.dtype)...  188 us
    dot_general x8, matrix products, product(): jnp.dot(left, right, precision=HIGH, preferred_element_type=jnp.float32)  64.7 us
    pallas_call x3, Pallas kernels, small_gather(): pl.pallas_call(kernel, out_shape=jax.ShapeDtypeStruct((count,) + block.sh...  40.6 us
    reduce_scatter x1, waiting for transfers between devices, shards(): lax.psum_scatter(grad_part, 'bvec', scatter_dimension=0, tiled=True)  32.4 us
  transfers between devices with their start and end apart: 2, of which 1 were waited for; matrix products, arithmetic and copies ran while one was open for 9% of the time, Pallas kernels for 5%

profile of v2, /device:TPU:0, one launch (start us, length us, event | category | flops | bytes accessed | tf_op | source)
XLA Modules:
  0.0 391.4 jit_solution(25818173837375123)
XLA Ops:
  7.6 2.9 select_reduce_fusion
  11.2 8.8 %shard_map.92 = f32[8,8,128]{2,1,0:T(8,128)} custom-call(f32[8,128]{1,0:T(8,128)} %reshape.156.block_ref), custom_call_target="tpu_custom_call" | custom-call | tf_op jit(solution)/shard_map/pallas_call | solution.py:75
  22.3 2.8 multiply_reduce_fusion.1
  29.4 1.8 multiply_reduce_fusion.4
  31.2 32.4 %reduce-scatter.2.cloned.1.call-done = f32[256,512]{1,0:T(8,128)} async-done(((f32[1024,512]{1,0:T(8,128)}), f32[256,512]{1,0:T(8,128)}) %reduce-scatter.2.cloned.1.call-update) | async-done | bytes 524304 | tf_op jit(solution)/shard_map/reduce_scatter | solution.py:270
  63.5 1.8 multiply_reduce_fusion.2
  65.3 2.7 stack.23
  68.6 11.4 %shard_map.93 = f32[32,8,128]{2,1,0:T(8,128)} custom-call(f32[8,128]{1,0:T(8,128)} %pad.4.block_ref), custom_call_target="tpu_custom_call" | custom-call | tf_op jit(solution)/shard_map/pallas_call | solution.py:75
  84.9 1.9 subtract_multiply_fusion.piece_ref
  86.8 92.9 %shard_map.94 = f32[2048,2048]{1,0:T(8,128)} custom-call(f32[256,512]{1,0:T(8,128)} %subtract_multiply_fusion.piece_ref), custom_call_target="tpu_custom_call" | custom-call | tf_op jit(solution)/shard_map/pallas_call | solution.py:185
  179.7 9.4 %fusion.7 = f32[64,2048]{1,0:T(8,128)S(1)} fusion(f32[2048,2048]{1,0:T(8,128)} %shard_map.94, s32[]{:T(128)S(6)} %select_n.37, s32[64]{0:T(128)S(1)} %iota_add_fusion.2), kind=kOutput, calls=%fused_computation.17 | convolution fusion | flops 1611661312 | bytes 17826820 | tf_op jit(solution)/shard_map/dot_general | solution.py:15
  190.4 6.0 %fusion.6 = f32[64,2048]{1,0:T(8,128)S(1)} fusion(f32[64,2048]{1,0:T(8,128)S(1)} %fusion.7, f32[2048,2048]{1,0:T(8,128)S(1)} %copy-done, s32[64]{0:T(128)S(1)} %iota_add_fusion.2), kind=kOutput, calls=%fused_computation.15 | convolution fusion | flops 1611137024 | bytes 17826048 | tf_op jit(solution)/shard_map/dot_general | solution.py:15
  196.4 6.0 %fusion.5 = f32[64,2048]{1,0:T(8,128)S(1)} fusion(f32[64,2048]{1,0:T(8,128)S(1)} %fusion.6, f32[2048,2048]{1,0:T(8,128)S(1)} %copy-done, s32[64]{0:T(128)S(1)} %iota_add_fusion.2), kind=kOutput, calls=%fused_computation.13 | convolution fusion | flops 1611137024 | bytes 17826048 | tf_op jit(solution)/shard_map/dot_general | solution.py:15
  202.4 6.2 %fusion.4 = f32[64,2048]{1,0:T(8,128)S(1)} fusion(f32[64,2048]{1,0:T(8,128)S(1)} %fusion.5, f32[2048,2048]{1,0:T(8,128)S(1)} %copy-done, s32[64]{0:T(128)S(1)} %iota_add_fusion.2), kind=kOutput, calls=%fused_computation.11 | convolution fusion | flops 1611137024 | bytes 17826048 | tf_op jit(solution)/shard_map/dot_general | solution.py:15
  208.5 6.0 %fusion.3 = f32[64,2048]{1,0:T(8,128)S(1)} fusion(f32[64,2048]{1,0:T(8,128)S(1)} %fusion.4, f32[2048,2048]{1,0:T(8,128)S(1)} %copy-done, s32[64]{0:T(128)S(1)} %iota_add_fusion.2), kind=kOutput, calls=%fused_computation.9 | convolution fusion | flops 1611137024 | bytes 17826048 | tf_op jit(solution)/shard_map/dot_general | solution.py:15
  214.5 6.0 %fusion.2 = f32[64,2048]{1,0:T(8,128)S(1)} fusion(f32[64,2048]{1,0:T(8,128)S(1)} %fusion.3, f32[2048,2048]{1,0:T(8,128)S(1)} %copy-done, s32[64]{0:T(128)S(1)} %iota_add_fusion.2), kind=kOutput, calls=%fused_computation.7 | convolution fusion | flops 1611137024 | bytes 17826048 | tf_op jit(solution)/shard_map/dot_general | solution.py:15
  220.5 7.0 %convolution_add_fusion.piece_ref = f32[64,2048]{1,0:T(8,128)} fusion(f32[64,2048]{1,0:T(8,128)S(1)} %fusion.2, f32[2048,2048]{1,0:T(8,128)S(1)} %copy-done, s32[64]{0:T(128)S(1)} %iota_add_fusion.2), kind=kOutput, calls=%fused_computation.5 | convolution fusion | flops 1611005952 | bytes 17826048 | tf_op jit(solution)/shard_map/dot_general | solution.py:15
  227.5 94.7 %shard_map.95 = f32[32,64,2048]{2,1,0:T(8,128)} custom-call(f32[64,2048]{1,0:T(8,128)} %convolution_add_fusion.piece_ref), custom_call_target="tpu_custom_call" | custom-call | tf_op jit(solution)/shard_map/pallas_call | solution.py:185
  322.3 4.1 %constant_dynamic-slice_fusion = f32[1024,2048]{1,0:T(8,128)S(1)} fusion(f32[2048,2048]{1,0:T(8,128)} %bitcast.45, s32[]{:T(128)S(6)} %select_n.34), kind=kLoop, calls=%fused_computation.50 | loop fusion | bytes 16777220 | tf_op jit(solution)/shard_map/dynamic_slice | solution.py:305
  326.9 18.2 %fusion = f32[2048,2048]{0,1:T(8,128)} fusion(f32[2048,512]{1,0:T(8,128)S(1)} %bitcast.48, f32[2048,2048]{1,0:T(8,128)} %bitcast.46, s32[]{:T(128)S(6)} %select_n.35), kind=kOutput, calls=%fused_computation.1 | convolution fusion | flops 12884901888 | bytes 25165828 | tf_op jit(solution)/shard_map/dot_general | solution.py:15
  345.1 7.5 %multiply_reduce_fusion = f32[2,2048]{1,0:T(2,128)S(1)} fusion(f32[1,2,1024,2048]{3,2,1,0:T(8,128)} %bitcast.47, f32[1024,2048]{1,0:T(8,128)S(1)} %constant_dynamic-slice_fusion), kind=kLoop, calls=%fused_computation | loop fusion | flops 8384512 | bytes 25182208 | tf_op jit(solution)/shard_map/reduce_sum | solution.py:309
  353.2 20.3 %shard_map.96 = f32[32,32,128]{2,1,0:T(8,128)} custom-call(f32[32,128]{1,0:T(8,128)} %reshape.162.block_ref), custom_call_target="tpu_custom_call" | custom-call | tf_op jit(solution)/shard_map/pallas_call | solution.py:75
  376.5 3.4 multiply_subtract_fusion
  379.9 3.1 copy.13
  (34 shorter events, 12.9 us)
Async XLA Ops:
  7.2 56.4 %reduce-scatter.2.cloned.1.call-start = ((), (), s32[]{:S(2)}) async-start(), calls=%async_computation.1 | async-start | bytes 2621440 | tf_op jit(solution)/shard_map/reduce_scatter | solution.py:270
  7.6 55.9 %copy-start.2 = (f32[1024,512]{1,0:T(8,128)S(1)}, f32[1024,512]{1,0:T(8,128)}, u32[]{:S(2)}) copy-start(f32[1024,512]{1,0:T(8,128)} %param.9) | copy-start | bytes 6291460
  27.4 349.1 %all-gather.2.cloned.1.call-start = ((), (), s32[]{:S(2)}) async-start(), calls=%async_computation.2 | async-start | bytes 2621440 | tf_op jit(solution)/shard_map/all_gather | solution.py:294
  179.7 10.7 %copy-start = (f32[2048,2048]{1,0:T(8,128)S(1)}, f32[2048,2048]{1,0:T(8,128)}, u32[]{:S(2)}) copy-start(f32[2048,2048]{1,0:T(8,128)} %shard_map.94) | copy-start | bytes 50331652
  322.3 4.6 %copy-start.1 = (f32[1,2,1024,512]{3,2,1,0:T(8,128)S(1)}, f32[1,2,1024,512]{3,2,1,0:T(8,128)}, u32[]{:S(2)}) copy-start(f32[1,2,1024,512]{3,2,1,0:T(8,128)} %param.5) | copy-start | bytes 12582916
  375.1 7.9 %copy-start.3 = (f32[4,2,2048]{2,1,0:T(2,128)}, f32[4,2,2048]{2,1,0:T(2,128)S(1)}, u32[]{:S(2)}) copy-start(f32[4,2,2048]{2,1,0:T(2,128)S(1)} %reduce_sum.135) | copy-start | bytes 196612
Sparse Core Ops, SparseCore 0:
  27.5 36.0 reduce-scatter.1
  322.4 36.7 all-gather.1
